TPU v7x, 128 devices: a whole 4x4x4 slice. The times are simulated.
128 devices in a mesh: prompts: 1, model: 16 (over z, y), resp: 8 (over x, core).
Axes of the slice: x: 4, y: 4, z: 4, core: 2. Of those that a mesh axis runs over, the one named last changes fastest.
Arguments:
- x_prompt: bfloat16 [1024, 4096], P(('prompts', 'resp'))
- x_resp: bfloat16 [8, 1024, 4096], P(('prompts', 'resp'))
- targets: int32 [8, 1024], P(('prompts', 'resp'))
- resp_lens: int32 [8], P(('prompts', 'resp'))
- attn_gain: float32 [2, 4096], replicated
- w_query: bfloat16 [2, 4096, 32, 128], P(None, None, 'model')
- w_key: bfloat16 [2, 4096, 32, 128], P(None, None, 'model')
- w_value: bfloat16 [2, 4096, 32, 128], P(None, None, 'model')
- w_out: bfloat16 [2, 32, 128, 4096], P(None, 'model')
- mlp_gain: float32 [2, 4096], replicated
- w_gate: bfloat16 [2, 4096, 11008], P(None, None, 'model')
- w_up: bfloat16 [2, 4096, 11008], P(None, None, 'model')
- w_down: bfloat16 [2, 11008, 4096], P(None, 'model')
- final_gain: float32 [4096], replicated
- w_vocab: bfloat16 [4096, 32768], P(None, 'model')
Outputs:
- output: float32 [8, 1024], P(('prompts', 'resp'))
All inputs are finite; a program needn't handle non-finite values.
Results may differ from a plain program's by a relative error of at most 0.002451.
Values are sent between devices in bfloat16 or wider.
A program may use at most 1 GiB of HBM per device.

v0:
```python
import functools

import jax
import jax.numpy as jnp
from jax import lax
from jax.experimental import pallas as pl
from jax.experimental.pallas import tpu as pltpu
from jax.sharding import PartitionSpec as P

MESH = pl.DeviceIdType.MESH
F32 = jnp.float32
BF16 = jnp.bfloat16
EPS = 1e-6
LANES = 128
PAIR = 2
RING = 4
COLUMNS = PAIR * LANES
SHARDS = RING * RING
BOTH = range(PAIR)
VMEM_BYTES = 67_000_000
LATE_ROWS = 640
LOGITS = 512
GROUP = 2
LAG = 4
VMEM = pl.BlockSpec(memory_space=pltpu.VMEM)
ANY = pl.BlockSpec(memory_space=pl.ANY)
DMA = pltpu.SemaphoreType.DMA
KINDS = range(RING * 3)
SUM_FAR, SUM_NEAR, SUM_RELAY, SUM2_FAR, SUM2_NEAR, SUM2_RELAY, TAKE_OWN, TAKE_REST, TAKE_RELAY, TAKE2_OWN, TAKE2_REST, TAKE2_RELAY = KINDS


def block_of(color, first, second):
    return RING * first + second if color else RING * second + first


def pair(index):
    return pl.ds(PAIR * index, PAIR)


class Torus:
    def __init__(self, refs, send_sem, recv_sem):
        self.refs = refs
        self.far, self.near, self.relayed, self.sums, self.relayed2, self.sums2, self.rows = refs
        self.send_sem, self.recv_sem = send_sem, recv_sem
        me = lax.axis_index("model")
        z, y = me // RING, me % RING
        self.place = ((y, z), (z, y))
        along_y = [z * RING + self.step(y, way) for way in (1, -1)]
        along_z = [self.step(z, way) * RING + y for way in (1, -1)]
        self.neighbors = ((along_y, along_z), (along_z, along_y))

    def step(self, place, by):
        return (place + by + RING) % RING

    def barrier(self):
        sem = pltpu.get_barrier_semaphore()
        for ring in self.neighbors[0]:
            for device in ring:
                pl.semaphore_signal(sem, device_id={"model": device}, device_id_type=MESH)
        pl.semaphore_wait(sem, RING)

    def ends(self, kind, c, q, d):
        (p, s), way, other = self.place[q], 1 - PAIR * d, 1 - d
        far, near, relayed, sums, relayed2, sums2, rows = (ref.at[c, q] for ref in self.refs)
        own = sums.at[0]
        back_s, back_p = self.step(s, -way), self.step(p, -way)
        return {
            SUM_FAR: lambda: (far.at[pair(d)], relayed.at[d], relayed.at[d]),
            SUM_NEAR: lambda: (near.at[d], sums.at[d, pair(other)], sums.at[d, pair(other)]),
            SUM_RELAY: lambda: (relayed.at[d], sums.at[d, pair(d)], sums.at[d, pair(d)]),
            SUM2_FAR: lambda: (own.at[self.step(s, PAIR), d], relayed2.at[d], relayed2.at[d]),
            SUM2_NEAR: lambda: (own.at[self.step(s, way), other], sums2.at[d, other], sums2.at[d, other]),
            SUM2_RELAY: lambda: (relayed2.at[d], sums2.at[d, d], sums2.at[d, d]),
            TAKE_OWN: lambda: (rows.at[p, s, d], rows.at[p, s, d], rows.at[p, back_s, d]),
            TAKE_REST: lambda: (rows.at[p, s, other], rows.at[p, s, other], rows.at[p, back_s, other]),
            TAKE_RELAY: lambda: (rows.at[p, back_s, d], rows.at[p, back_s, d], rows.at[p, self.step(s, PAIR), d]),
            TAKE2_OWN: lambda: (rows.at[p, pair(d)], rows.at[p, pair(d)], rows.at[back_p, pair(d)]),
            TAKE2_REST: lambda: (rows.at[p, pair(other)], rows.at[p, pair(other)], rows.at[back_p, pair(other)]),
            TAKE2_RELAY: lambda: (rows.at[back_p, pair(d)], rows.at[back_p, pair(d)], rows.at[self.step(p, PAIR), pair(d)]),
        }[kind]()

    def copy(self, kind, c, q, d, src, dst):
        second_ring = kind in (SUM2_FAR, SUM2_NEAR, SUM2_RELAY, TAKE_OWN, TAKE_REST, TAKE_RELAY)
        return pltpu.make_async_remote_copy(
            src_ref=src, dst_ref=dst, send_sem=self.send_sem.at[c, q, d, kind], recv_sem=self.recv_sem.at[c, q, d, kind],
            device_id={"model": self.neighbors[q][second_ring][d]}, device_id_type=MESH)

    def send(self, c, q, d, kind):
        src, dst, _ = self.ends(kind, c, q, d)
        self.copy(kind, c, q, d, src, dst).start()

    def sent(self, c, q, *kinds):
        for kind in kinds:
            for d in BOTH:
                src, dst, _ = self.ends(kind, c, q, d)
                self.copy(kind, c, q, d, src, dst).wait_send()

    def arrived(self, c, q, d, *kinds):
        for kind in kinds:
            _, _, here = self.ends(kind, c, q, d)
            self.copy(kind, c, q, d, here, here).wait_recv()


def halves(value):
    return value[:, :LANES], value[:, LANES:]


def store_block(ref, value):
    for half, part in enumerate(halves(value)):
        ref[half] = part


def add_block(ref, value):
    for half, part in enumerate(halves(value)):
        ref[half] += part


class Stage:
    def __init__(self, net, lhs_of, w_ref, finish):
        self.net, self.lhs_of, self.w_ref, self.finish = net, lhs_of, w_ref, finish

    def product(self, lhs, color, first, second):
        start = pl.multiple_of(block_of(color, first, second) * COLUMNS, COLUMNS)
        return jnp.dot(lhs, self.w_ref[:, pl.ds(start, COLUMNS)], preferred_element_type=F32)

    def begin(self, c, q):
        net, p, lhs = self.net, self.net.place[q][0], self.lhs_of(c, q)
        for k in range(RING):
            store_block(net.far.at[c, q, k], self.product(lhs, q, net.step(p, PAIR), k))
        for d in BOTH:
            net.send(c, q, d, SUM_FAR)
        for d in BOTH:
            for k in BOTH:
                store_block(net.near.at[c, q, d, k], self.product(lhs, q, net.step(p, 1 - PAIR * d), PAIR * (1 - d) + k))
            net.send(c, q, d, SUM_NEAR)

    def relay_sum(self, c, q):
        net, p, lhs = self.net, self.net.place[q][0], self.lhs_of(c, q)
        for d in BOTH:
            net.arrived(c, q, d, SUM_FAR)
            for k in BOTH:
                add_block(net.relayed.at[c, q, d, k], self.product(lhs, q, net.step(p, 1 - PAIR * d), PAIR * d + k))
            net.send(c, q, d, SUM_RELAY)

    def begin_second(self, c, q):
        net, lhs = self.net, self.lhs_of(c, q)
        for d in BOTH:
            net.arrived(c, q, d, SUM_NEAR, SUM_RELAY)
        for k in range(RING):
            for half, part in enumerate(halves(self.product(lhs, q, net.place[q][0], k))):
                net.sums[c, q, 0, k, half] += net.sums[c, q, 1, k, half] + part
        for kind in (SUM2_FAR, SUM2_NEAR):
            for d in BOTH:
                net.send(c, q, d, kind)
        net.sent(c, q, SUM_FAR)

    def relay_second(self, c, q):
        net = self.net
        for d in BOTH:
            net.arrived(c, q, d, SUM2_FAR)
            net.relayed2[c, q, d] += net.sums[c, q, 0, net.step(net.place[q][1], 1 - PAIR * d), d]
            net.send(c, q, d, SUM2_RELAY)

    def finish_sum(self, c, q):
        net = self.net
        net.sent(c, q, SUM_NEAR, SUM_RELAY)
        for d in BOTH:
            net.arrived(c, q, d, SUM2_NEAR, SUM2_RELAY)
        for half in BOTH:
            self.finish(c, q, half, net.sums[c, q, 0, net.place[q][1], half] + net.sums2[c, q, 0, half] + net.sums2[c, q, 1, half])
        for kind in (TAKE_OWN, TAKE_REST):
            for d in BOTH:
                net.send(c, q, d, kind)

    def relay_rows(self, c, q):
        net = self.net
        net.sent(c, q, SUM2_FAR, SUM2_NEAR, SUM2_RELAY)
        for d in BOTH:
            net.arrived(c, q, d, TAKE_OWN)
            net.send(c, q, d, TAKE_RELAY)

    def take_second(self, c, q):
        net = self.net
        for d in BOTH:
            net.arrived(c, q, d, TAKE_REST, TAKE_RELAY)
        for kind in (TAKE2_OWN, TAKE2_REST):
            for d in BOTH:
                net.send(c, q, d, kind)

    def relay_last(self, c, q):
        net = self.net
        for d in BOTH:
            net.arrived(c, q, d, TAKE2_OWN)
            net.send(c, q, d, TAKE2_RELAY)

    def complete(self, c, q):
        net = self.net
        for d in BOTH:
            net.arrived(c, q, d, TAKE2_REST, TAKE2_RELAY)
        net.sent(c, q, TAKE_OWN, TAKE_REST, TAKE_RELAY, TAKE2_OWN, TAKE2_REST, TAKE2_RELAY)

    def middle(self):
        return [self.relay_sum, self.begin_second, self.relay_second, self.finish_sum, self.relay_rows, self.take_second, self.relay_last]


def normed(net, c, q, gain_ref):
    rows = net.rows.shape[-PAIR]
    tile = PAIR * 8 if rows % (PAIR * 8) == 0 else 8
    spots = [(first, second, half) for first in range(RING) for second in range(RING) for half in BOTH]

    @pl.loop(0, rows // tile)
    def _(i):
        span = pl.ds(pl.multiple_of(i * tile, tile), tile)
        acts = [net.rows[(c, q) + spot + (span,)].astype(F32) for spot in spots]
        squares = functools.reduce(jnp.add, [v * v for v in acts])
        inv = lax.rsqrt(jnp.sum(squares, axis=-1, keepdims=True) / (LANES * len(acts)) + EPS)
        for k, (spot, v) in enumerate(zip(spots, acts)):
            net.rows[(c, q) + spot + (span,)] = (v * inv * gain_ref[q, pl.ds(k, 1)]).astype(BF16)


def rows_of(net, c, q):
    parts = []
    for upper in range(RING):
        for lower in range(RING):
            first, second = (upper, lower) if q else (lower, upper)
            parts += [net.rows[c, q, first, second, half] for half in BOTH]
    return jnp.concatenate(parts, axis=1)


def times_transposed(lhs, rhs):
    return lax.dot_general(lhs, rhs, (((1,), (1,)), ((), ())), preferred_element_type=F32)


def late_plan(width, count):
    plan, start = [], 0
    for buffer in BOTH:
        for slot in range(width // count):
            size = min(LATE_ROWS, width - start)
            if size:
                plan.append((buffer, slot * count, start, size))
            start += size
    return plan, width - start


def rope(value, cos, sin):
    return jnp.concatenate([v * cos + pltpu.roll(v, LANES // PAIR, 1) * sin for v in halves(value)], axis=1)


def put_projected(product, cos_ref, sin_ref, out_ref, c, q):
    for k in range(3):
        value = product(k * COLUMNS, COLUMNS)
        if k < PAIR:
            value = rope(value, cos_ref[c, q], sin_ref[c, q])
        out_ref[c, q, :, pl.ds(k * COLUMNS, COLUMNS)] = value.astype(BF16)


def put_statistics(product, count, target_ref, out_ref, c, q):
    top = total = picked = None
    for k in range(count // LOGITS):
        logits = product(k * LOGITS, LOGITS)
        here = jnp.max(logits, axis=-1, keepdims=True)
        ids = lax.broadcasted_iota(jnp.int32, logits.shape, 1) + k * LOGITS
        found = jnp.sum(jnp.where(ids == target_ref[c, q, :, :1], logits, 0.0), axis=-1, keepdims=True)
        if k:
            both = jnp.maximum(top, here)
            total = total * jnp.exp(top - both) + jnp.sum(jnp.exp(logits - both), axis=-1, keepdims=True)
            top, picked = both, picked + found
        else:
            top, total, picked = here, jnp.sum(jnp.exp(logits - here), axis=-1, keepdims=True), found
    lane = lax.broadcasted_iota(jnp.int32, out_ref.shape[PAIR:], 1)
    out_ref[c, q] = jnp.where(lane == 0, top, jnp.where(lane == 1, total, picked))


def mega_kernel(chunks, layer, last, a_ref, res_ref, gain_ref, next_gain_ref, *args):
    side_refs, args = args[:PAIR - last], args[PAIR - last:]
    (w_out_hbm, w_gate_hbm, w_up_hbm, w_down_hbm, late_hbm, out_ref, new_res_ref,
     w_out, w_gate, w_up, w_down, late_rest, inner, middle,
     far, near, relayed, sums, relayed2, sums2, rows, w_sem, late_sem, send_sem, recv_sem) = args
    loads = [pltpu.make_async_copy(src.at[layer], dst, w_sem.at[i]) for i, (src, dst) in enumerate(
        ((w_out_hbm, w_out), (w_gate_hbm, w_gate), (w_up_hbm, w_up), (w_down_hbm, w_down)))]
    for load in loads:
        load.start()
    width, count = late_hbm.shape
    plan, left = late_plan(width, count)
    late = [(late_hbm.at[pl.ds(start, size)], (w_gate, w_up)[buffer].at[pl.ds(0, size), pl.ds(lane, count)]) for buffer, lane, start, size in plan]
    if left:
        late.append((late_hbm.at[pl.ds(width - left, left)], late_rest))
    late_loads = [pltpu.make_async_copy(src, dst, late_sem.at[i]) for i, (src, dst) in enumerate(late)]
    net = Torus((far, near, relayed, sums, relayed2, sums2, rows), send_sem, recv_sem)
    net.barrier()
    loads[0].wait()

    def finish_with(old_ref, new_ref):
        def finish(c, q, half, total):
            value = (old_ref[c, q, half].astype(F32) + total).astype(BF16)
            new_ref[c, q, half] = value
            rows[(c, q) + net.place[q] + (half,)] = value
        return finish

    first = Stage(net, lambda c, q: a_ref[c, q], w_out, finish_with(res_ref, middle))
    second = Stage(net, lambda c, q: inner[c, q], w_down, finish_with(middle, new_res_ref))

    def mlp(c, q):
        first.complete(c, q)
        normed(net, c, q, gain_ref)
        hidden = rows_of(net, c, q)
        inner[c, q] = (jax.nn.silu(times_transposed(hidden, w_gate[...])) * times_transposed(hidden, w_up[...])).astype(BF16)
        second.begin(c, q)

    def after(c, q):
        second.complete(c, q)
        normed(net, c, q, next_gain_ref)
        hidden = rows_of(net, c, q)

        def product(lane, size):
            parts = [jnp.dot(hidden[:, start:start + rows_here], (w_gate, w_up)[buffer][pl.ds(0, rows_here), pl.ds(at + lane, size)], preferred_element_type=F32)
                     for buffer, at, start, rows_here in plan]
            if left:
                parts.append(jnp.dot(hidden[:, width - left:], late_rest[:, pl.ds(lane, size)], preferred_element_type=F32))
            return functools.reduce(jnp.add, parts)

        if last:
            put_statistics(product, count, *side_refs, out_ref, c, q)
        else:
            put_projected(product, *side_refs, out_ref, c, q)

    steps = [first.begin, *first.middle(), mlp, *second.middle(), after]
    groups = [(at, min(at + GROUP, chunks)) for at in range(0, chunks, GROUP)]
    final = len(groups) - 1

    def run(step, group):
        if step == mlp and group == 0:
            for load in loads[1:]:
                load.wait()
        if step == after and group == 0:
            for load in late_loads:
                load.wait()

        @pl.loop(*groups[group])
        def _(c):
            for q in BOTH:
                step(c, q)

        if step == mlp and group == final:
            for load in late_loads:
                load.start()

    for slot in range(len(steps) + LAG * final):
        for group in range(len(groups)):
            if 0 <= slot - LAG * group < len(steps):
                run(steps[slot - LAG * group], group)


def mega(a, res, gain, next_gain, sides, w_out, w_gate_t, w_up_t, w_down, late, layer, collective_id):
    chunks, _, rows, depth = a.shape
    _, hidden, width = w_gate_t.shape
    per = (chunks, PAIR)
    tile = (rows, LANES)
    last = len(sides) == 1
    count = late.shape[1]
    _, left = late_plan(width, count)

    def by_color(g):
        grid = g.reshape(RING, RING, PAIR, LANES)
        return jnp.stack([jnp.swapaxes(grid, 0, 1), grid]).reshape(PAIR, PAIR * SHARDS, LANES)

    sem = DMA(per + (PAIR, len(KINDS)))
    out = jax.ShapeDtypeStruct(per + tile, F32) if last else jax.ShapeDtypeStruct(per + (rows, count), BF16)
    return pl.pallas_call(
        functools.partial(mega_kernel, chunks, layer, last),
        out_shape=(out, jax.ShapeDtypeStruct(per + (PAIR,) + tile, BF16)),
        in_specs=[VMEM] * (4 + len(sides)) + [ANY] * 5,
        out_specs=(VMEM, VMEM),
        scratch_shapes=[
            pltpu.VMEM((depth, width), BF16),
            *[pltpu.VMEM((hidden, width), BF16) for _ in range(3)],
            pltpu.VMEM((left or 8, count), BF16),
            pltpu.VMEM(per + (rows, hidden), BF16),
            pltpu.VMEM(per + (PAIR,) + tile, BF16),
            pltpu.VMEM(per + (RING, PAIR) + tile, F32),
            pltpu.VMEM(per + (PAIR, PAIR, PAIR) + tile, F32),
            pltpu.VMEM(per + (PAIR, PAIR, PAIR) + tile, F32),
            pltpu.VMEM(per + (PAIR, RING, PAIR) + tile, F32),
            pltpu.VMEM(per + (PAIR,) + tile, F32),
            pltpu.VMEM(per + (PAIR, PAIR) + tile, F32),
            pltpu.VMEM(per + (RING, RING, PAIR) + tile, BF16),
            DMA((RING,)), DMA((SHARDS,)), sem, sem,
        ],
        compiler_params=pltpu.CompilerParams(collective_id=collective_id, has_side_effects=True, vmem_limit_bytes=VMEM_BYTES),
        name=f"mega{collective_id}",
    )(a, res, by_color(gain), by_color(next_gain), *sides, w_out, w_gate_t, w_up_t, w_down, late)


PEERS = 8
TILE = 128
Q_TILE = 256
LOG2E = 1.4426950408889634
HELD = pltpu.VMEM((PEERS, PAIR, TILE, COLUMNS), BF16)
GATHER_SEMS = [DMA((PAIR, 3)), DMA((PAIR, 3)), DMA((RING,)), DMA((RING,))]


class Exchange:
    def __init__(self):
        self.me = lax.axis_index("resp")
        self.others = [(self.me + k) % PEERS for k in range(1, PEERS)]

    def barrier(self):
        sem = pltpu.get_barrier_semaphore()
        for device in self.others:
            pl.semaphore_signal(sem, inc=1, device_id={"resp": device}, device_id_type=MESH)
        pl.semaphore_wait(sem, PEERS - 1)

    def copy(self, src, dst, send_sem, recv_sem, device):
        return pltpu.make_async_remote_copy(src_ref=src, dst_ref=dst, send_sem=send_sem, recv_sem=recv_sem,
                                            device_id={"resp": device}, device_id_type=MESH)

    def scatter(self, src_of, dst, send_sem, recv_sem):
        for device in self.others:
            self.copy(src_of(device), dst, send_sem.at[device], recv_sem.at[self.me], device).start()

    def collected(self, dst_of, recv_sem):
        for device in self.others:
            self.copy(dst_of(device), dst_of(device), recv_sem.at[device], recv_sem.at[device], device).wait_recv()

    def sent(self, src_of, send_sem, recv_sem):
        for device in self.others:
            self.copy(src_of(device), src_of(device), send_sem.at[device], recv_sem.at[device], device).wait_send()


class PromptGather:
    def __init__(self, net, held, ring_send, ring_recv, near_send, near_recv):
        self.net, self.held = net, held
        self.ring_sems, self.near_sems = (ring_send, ring_recv), (near_send, near_recv)
        x, core = net.me // PAIR, net.me % PAIR
        self.at = lambda by, here: (x + by + RING) % RING * PAIR + (core if here else 1 - core)

    def ring_copy(self, d, kind, ref):
        return self.net.copy(ref, ref, self.ring_sems[0].at[d, kind], self.ring_sems[1].at[d, kind], self.at(1 - PAIR * d, True))

    def near_copy(self, kind, ref):
        return self.net.copy(ref, ref, self.near_sems[0].at[kind], self.near_sems[1].at[kind], self.at(0, False))

    def sources(self, here):
        return [self.at(by, here) for by in (0, -1, 1, PAIR)]

    def start(self):
        own = self.held.at[self.net.me]
        for kind in BOTH:
            for d in BOTH:
                self.ring_copy(d, kind, own.at[1 - d if kind else d]).start()
        self.near_copy(0, own).start()

    def relay(self):
        for d in BOTH:
            ref = self.held.at[self.at(PAIR * d - 1, True), d]
            self.ring_copy(d, 0, ref).wait_recv()
            self.ring_copy(d, PAIR, ref).start()

    def share(self):
        for d in BOTH:
            device = self.at(PAIR * d - 1, True)
            self.ring_copy(d, 1, self.held.at[device, 1 - d]).wait_recv()
            self.near_copy(1 + d, self.held.at[device]).start()
        far = self.held.at[self.at(PAIR, True)]
        for d in BOTH:
            self.ring_copy(d, PAIR, far.at[d]).wait_recv()
        self.near_copy(3, far).start()

    def collect(self):
        for kind, device in enumerate(self.sources(False)):
            self.near_copy(kind, self.held.at[device]).wait_recv()

    def finish(self):
        for kind in range(3):
            for d in BOTH:
                self.ring_copy(d, kind, self.held.at[self.net.me, d]).wait_send()
        for kind in range(RING):
            self.near_copy(kind, self.held.at[self.net.me]).wait_send()


def deal(rows):
    out = lax.broadcasted_iota(jnp.int32, (rows, rows), 0)
    src = lax.broadcasted_iota(jnp.int32, (rows, rows), 1)
    per = rows // PEERS
    return jnp.where(src == (out % per) * PEERS + out // per, 1.0, 0.0).astype(BF16)


def undeal(rows):
    out = lax.broadcasted_iota(jnp.int32, (rows, rows), 0)
    src = lax.broadcasted_iota(jnp.int32, (rows, rows), 1)
    per = rows // PEERS
    return jnp.where(src == (out % PEERS) * per + out // PEERS, 1.0, 0.0).astype(BF16)


def norm_tile(x_ref, out_ref, gain_ref):
    for i in range(x_ref.shape[0] // 16):
        v = x_ref[pl.ds(16 * i, 16), :].astype(F32)
        inv = lax.rsqrt(jnp.mean(v * v, axis=-1, keepdims=True) + EPS)
        out_ref[pl.ds(16 * i, 16), :] = (v * inv * gain_ref[...]).astype(BF16)


def softmax_mix(q, pieces):
    factor = LOG2E * 128 ** -0.5
    outs = []
    for h in range(2):
        lanes = slice(128 * h, 128 * h + 128)
        scores = []
        for keys, _, mask in pieces:
            s = lax.dot_general(q[:, lanes], keys[:, lanes], (((1,), (1,)), ((), ())), preferred_element_type=F32)
            scores.append(s if mask is None else jnp.where(mask, s, -jnp.inf))
        top = functools.reduce(jnp.maximum, [jnp.max(s, axis=-1, keepdims=True) for s in scores])
        probs = [jnp.exp2((s - top) * factor) for s in scores]
        total = functools.reduce(jnp.add, [jnp.sum(p, axis=-1, keepdims=True) for p in probs])
        mixed = functools.reduce(jnp.add, [jnp.dot(p.astype(BF16), values[:, lanes], preferred_element_type=F32) for p, (_, values, _) in zip(probs, pieces)])
        outs.append(mixed / total)
    return jnp.concatenate(outs, axis=1).astype(BF16)


def prompt_rows_of(held, which):
    return held[:, which].reshape(PEERS * TILE, COLUMNS)


def attend_response(t, q, held, k_own, v_own):
    row = lax.broadcasted_iota(jnp.int32, (Q_TILE, Q_TILE), 0)
    col = lax.broadcasted_iota(jnp.int32, (Q_TILE, Q_TILE), 1)
    pieces = [(prompt_rows_of(held, 0), prompt_rows_of(held, 1), None)]
    if t:
        pieces.append((k_own[:t * Q_TILE], v_own[:t * Q_TILE], None))
    span = slice(t * Q_TILE, (t + 1) * Q_TILE)
    pieces.append((k_own[span], v_own[span], col <= row))
    return softmax_mix(q, pieces)


def deal_mixed(net, t, mixed, stage, out, send_sem, recv_sem):
    dealt = jnp.dot(deal(Q_TILE), mixed, preferred_element_type=F32).astype(BF16)
    stage[t] = dealt.reshape(PEERS, Q_TILE // PEERS, COLUMNS)
    net.scatter(lambda d: stage.at[t, d], out.at[net.me, t], send_sem.at[t], recv_sem.at[t])
    out[net.me, t] = stage[t, net.me]


def first_attention_kernel(xp_hbm, xr_hbm, wq_hbm, wk_hbm, wv_hbm, gain_ref, cos_ref, sin_ref, info_ref,
                           mixed_out, res_out, info_out, prompt_out,
                           xs, w, hidden, q_s, k_s, v_s, held, mixed_stage, res_stage,
                           x_sem, w_sem, ring_send, ring_recv, near_send, near_recv, mix_send, mix_recv, res_send, res_recv, info_send, info_recv):
    net = Exchange()
    prompt = PromptGather(net, held, ring_send, ring_recv, near_send, near_recv)
    me = net.me
    column = pl.multiple_of(lax.axis_index("model") * COLUMNS, COLUMNS)

    def load(t):
        src = xp_hbm if isinstance(t, int) and t == 0 else xr_hbm.at[pl.ds(pl.multiple_of((t - 1) * TILE, TILE), TILE)]
        return pltpu.make_async_copy(src, xs.at[t], x_sem.at[t])

    load(0).start()
    weights = [pltpu.make_async_copy(src, w.at[:, pl.ds(COLUMNS * i, COLUMNS)], w_sem.at[i]) for i, src in enumerate((wq_hbm, wk_hbm, wv_hbm))]
    for copy in weights:
        copy.start()
    for t in range(1, 9):
        load(t).start()
    net.barrier()
    net.scatter(lambda d: info_ref.at[d], info_out.at[me], info_send, info_recv)
    info_out[me] = info_ref[me]

    def project(t):
        span = pl.ds(pl.multiple_of(t * TILE, TILE), TILE)
        qkv = jnp.dot(hidden[t % 2], w[...], preferred_element_type=F32)
        cos, sin = cos_ref[span], sin_ref[span]
        return span, rope(qkv[:, :COLUMNS], cos, sin).astype(BF16), rope(qkv[:, COLUMNS:512], cos, sin).astype(BF16), qkv[:, 512:].astype(BF16)

    load(0).wait()
    norm_tile(xs.at[0], hidden.at[0], gain_ref)
    load(1).wait()
    for copy in weights:
        copy.wait()
    norm_tile(xs.at[1], hidden.at[1], gain_ref)
    span, q, k, v = project(0)
    q_s[span] = q
    held[me, 0] = k
    held[me, 1] = v
    prompt.start()
    spread = deal(TILE)

    @pl.loop(1, 9)
    def _(t):
        later = jnp.minimum(t + 1, 8)

        @pl.when(t < 8)
        def _():
            load(t + 1).wait()

        span, q, k, v = project(t)
        norm_tile(xs.at[later], hidden.at[(t + 1) % 2], gain_ref)
        q_s[span] = q
        own = pl.ds(pl.multiple_of((t - 1) * TILE, TILE), TILE)
        k_s[own] = k
        v_s[own] = v
        dealt = jnp.dot(spread, xs[t, :, pl.ds(column, COLUMNS)], preferred_element_type=F32).astype(BF16)
        res_stage[:, t - 1] = dealt.reshape(PEERS, TILE // PEERS, COLUMNS)
        pl.when(t == 3)(prompt.relay)
        pl.when(t == 5)(prompt.share)

    net.scatter(lambda d: res_stage.at[d], res_out.at[me], res_send, res_recv)
    res_out[me] = res_stage[me]
    prompt.collect()
    for t in range(RING):
        mixed = attend_response(t, q_s[pl.ds(TILE + t * Q_TILE, Q_TILE)], held, k_s, v_s)
        deal_mixed(net, t, mixed, mixed_stage, mixed_out, mix_send, mix_recv)
    row = lax.broadcasted_iota(jnp.int32, (TILE, PEERS * TILE), 0) + me * TILE
    col = lax.broadcasted_iota(jnp.int32, (TILE, PEERS * TILE), 1)
    prompt_out[:, :COLUMNS] = softmax_mix(q_s[pl.ds(0, TILE)], [(prompt_rows_of(held, 0), prompt_rows_of(held, 1), col <= row)])
    prompt_out[:, COLUMNS:] = xs[0, :, pl.ds(column, COLUMNS)]
    finish_exchange(net, mixed_stage, mixed_out, mix_send, mix_recv)
    net.collected(lambda d: res_out.at[d], res_recv)
    net.sent(lambda d: res_stage.at[d], res_send, res_recv)
    net.collected(lambda d: info_out.at[d], info_recv)
    net.sent(lambda d: info_ref.at[d], info_send, info_recv)
    prompt.finish()


def finish_exchange(net, stage, out, send_sem, recv_sem):
    for t in range(RING):
        net.collected(lambda d: out.at[d, t], recv_sem.at[t])
        net.sent(lambda d: stage.at[t, d], send_sem.at[t], recv_sem.at[t])


def first_attention(x_prompt, x_resp, w_query, w_key, w_value, gain, cos, sin, info, collective_id):
    rows = TILE + x_resp.shape[0]
    width = x_resp.shape[1]
    return pl.pallas_call(
        first_attention_kernel,
        out_shape=(jax.ShapeDtypeStruct((PEERS, RING, 32, COLUMNS), BF16), jax.ShapeDtypeStruct((PEERS, 8, 16, COLUMNS), BF16),
                   jax.ShapeDtypeStruct((PEERS, 8, 128), jnp.int32), jax.ShapeDtypeStruct((TILE, PAIR * COLUMNS), BF16)),
        in_specs=[ANY] * 5 + [VMEM] * 4,
        out_specs=(VMEM,) * 4,
        scratch_shapes=[
            pltpu.VMEM((9, TILE, width), BF16), pltpu.VMEM((width, 768), BF16), pltpu.VMEM((2, TILE, width), BF16),
            pltpu.VMEM((rows, COLUMNS), BF16), pltpu.VMEM((rows - TILE, COLUMNS), BF16), pltpu.VMEM((rows - TILE, COLUMNS), BF16),
            HELD, pltpu.VMEM((RING, PEERS, 32, COLUMNS), BF16), pltpu.VMEM((PEERS, 8, 16, COLUMNS), BF16),
            DMA((9,)), DMA((3,)), *GATHER_SEMS, DMA((RING, PEERS)), DMA((RING, PEERS)), *[DMA((PEERS,)) for _ in range(RING)],
        ],
        compiler_params=pltpu.CompilerParams(collective_id=collective_id, has_side_effects=True, vmem_limit_bytes=VMEM_BYTES),
        name="first_attention",
    )(x_prompt, x_resp, w_query, w_key, w_value, gain.reshape(1, width), cos, sin, info)


def second_attention_kernel(qkv_ref, kv_prompt_ref, mixed_out, qkv_in, k_s, v_s, held, mixed_stage,
                            ring_send, ring_recv, near_send, near_recv, qkv_send, qkv_recv, mix_send, mix_recv):
    net = Exchange()
    me = net.me
    prompt = PromptGather(net, held, ring_send, ring_recv, near_send, near_recv)
    held[me] = kv_prompt_ref[...]
    net.barrier()
    prompt.start()

    def send_rows(t):
        net.scatter(lambda d: qkv_ref.at[t, d], qkv_in.at[t, me], qkv_send.at[t], qkv_recv.at[t])
        qkv_in[t, me] = qkv_ref[t, me]

    send_rows(0)
    prompt.relay()
    prompt.share()
    for t in range(1, RING):
        send_rows(t)
    prompt.collect()
    for t in range(RING):
        net.collected(lambda d: qkv_in.at[t, d], qkv_recv.at[t])
        rows = jnp.dot(undeal(Q_TILE), qkv_in[t].reshape(Q_TILE, 3 * COLUMNS), preferred_element_type=F32).astype(BF16)
        k_s[pl.ds(t * Q_TILE, Q_TILE)] = rows[:, COLUMNS:PAIR * COLUMNS]
        v_s[pl.ds(t * Q_TILE, Q_TILE)] = rows[:, PAIR * COLUMNS:]
        mixed = attend_response(t, rows[:, :COLUMNS], held, k_s, v_s)
        deal_mixed(net, t, mixed, mixed_stage, mixed_out, mix_send, mix_recv)
    finish_exchange(net, mixed_stage, mixed_out, mix_send, mix_recv)
    for t in range(RING):
        net.sent(lambda d: qkv_ref.at[t, d], qkv_send.at[t], qkv_recv.at[t])
    prompt.finish()


def second_attention(qkv, kv_prompt, collective_id):
    rows = RING * Q_TILE
    return pl.pallas_call(
        second_attention_kernel,
        out_shape=jax.ShapeDtypeStruct((PEERS, RING, 32, COLUMNS), BF16),
        in_specs=[VMEM, VMEM],
        out_specs=VMEM,
        scratch_shapes=[
            pltpu.VMEM((RING, PEERS, 32, 3 * COLUMNS), BF16), pltpu.VMEM((rows, COLUMNS), BF16), pltpu.VMEM((rows, COLUMNS), BF16),
            HELD, pltpu.VMEM((RING, PEERS, 32, COLUMNS), BF16), *GATHER_SEMS, *[DMA((RING, PEERS)) for _ in range(RING)],
        ],
        compiler_params=pltpu.CompilerParams(collective_id=collective_id, has_side_effects=True, vmem_limit_bytes=VMEM_BYTES),
        name=f"second_attention{collective_id}",
    )(qkv, kv_prompt)


def combine_kernel(shards, stats_ref, out_ref, every, stat_send, stat_recv, row_send, row_recv):
    me, home = lax.axis_index("model"), lax.axis_index("resp")
    sem = pltpu.get_barrier_semaphore()
    models = [(me + k) % shards for k in range(1, shards)]
    homes = [(home + k) % PEERS for k in range(1, PEERS)]
    for device in models:
        pl.semaphore_signal(sem, inc=1, device_id={"model": device}, device_id_type=MESH)
    for device in homes:
        pl.semaphore_signal(sem, inc=1, device_id={"resp": device}, device_id_type=MESH)
    pl.semaphore_wait(sem, shards + PEERS - 2)

    def stat_copy(src, dst, send, recv, device):
        return pltpu.make_async_remote_copy(src_ref=src, dst_ref=dst, send_sem=send, recv_sem=recv, device_id={"model": device}, device_id_type=MESH)

    def row_copy(src, dst, send, recv, device):
        return pltpu.make_async_remote_copy(src_ref=src, dst_ref=dst, send_sem=send, recv_sem=recv, device_id={"resp": device}, device_id_type=MESH)

    for device in models:
        stat_copy(stats_ref, every.at[me], stat_send.at[device], stat_recv.at[me], device).start()
    every[me] = stats_ref[...]
    for device in models:
        stat_copy(every.at[device], every.at[device], stat_send.at[device], stat_recv.at[device], device).wait_recv()
    tops = [every[k, 0] for k in range(shards)]
    top = functools.reduce(jnp.maximum, tops)
    total = functools.reduce(jnp.add, [every[k, 1] * jnp.exp(tops[k] - top) for k in range(shards)])
    picked = functools.reduce(jnp.add, [every[k, 2] for k in range(shards)])
    out_ref[home] = picked - top - jnp.log(total)
    for device in homes:
        row_copy(out_ref.at[home], out_ref.at[home], row_send.at[device], row_recv.at[home], device).start()
    for device in homes:
        row_copy(out_ref.at[device], out_ref.at[device], row_send.at[device], row_recv.at[device], device).wait_recv()
    for device in models:
        stat_copy(stats_ref, stats_ref, stat_send.at[device], stat_recv.at[device], device).wait_send()
    for device in homes:
        row_copy(out_ref.at[home], out_ref.at[home], row_send.at[device], row_recv.at[device], device).wait_send()


def combine(stats, shards, collective_id):
    return pl.pallas_call(
        functools.partial(combine_kernel, shards),
        out_shape=jax.ShapeDtypeStruct((PEERS, 8, 128), F32),
        in_specs=[VMEM],
        out_specs=VMEM,
        scratch_shapes=[pltpu.VMEM((shards, 3, 8, 128), F32), DMA((shards,)), DMA((shards,)), DMA((PEERS,)), DMA((PEERS,))],
        compiler_params=pltpu.CompilerParams(collective_id=collective_id, has_side_effects=True),
        name=f"combine{collective_id}",
    )(stats)


ROPE_BASE = 10000.0
VARIANTS = (704, 1024)
CHUNKS = 4


def rope_tables(positions):
    half = LANES // PAIR
    frequency = ROPE_BASE ** (-jnp.arange(half, dtype=F32) / half)
    angles = positions.astype(F32)[:, None] * frequency
    cos, sin = jnp.cos(angles), jnp.sin(angles)
    return jnp.concatenate([cos, cos], axis=1), jnp.concatenate([-sin, sin], axis=1)


def by_chunk(rows):
    return rows.reshape(CHUNKS, PAIR, rows.shape[0] // (CHUNKS * PAIR), rows.shape[1])


def to_blocks(rows):
    grid = by_chunk(rows)
    return jnp.swapaxes(grid.reshape(grid.shape[:3] + (PAIR, LANES)), 2, 3)


def from_blocks(blocks):
    return jnp.swapaxes(blocks, 2, 3).reshape(-1, COLUMNS)


def solution(mesh):
    groups = mesh.shape['resp']
    shards = mesh.shape['model']
    row_axes = ('prompts', 'resp')
    head_spec = P(None, None, 'model', None)
    in_specs = (P(row_axes, None), P(row_axes, None, None), P(row_axes, None), P(row_axes), P(None, None), head_spec, head_spec, head_spec, P(None, 'model', None, None), P(None, None), P(None, None, 'model'), P(None, None, 'model'), P(None, 'model', None), P(None), P(None, 'model'))

    def device_step(x_prompt, x_resp, targets, resp_lens, attn_gain, w_query, w_key, w_value, w_out, mlp_gain, w_gate, w_up, w_down, final_gain, w_vocab):
        prompt_rows = x_prompt.shape[0]
        resp_len, width = x_resp.shape[1:]
        prompt_len = prompt_rows * groups
        me = lax.axis_index('model')
        home = lax.axis_index('resp')
        per = resp_len // groups
        gate_t, up_t = jnp.swapaxes(w_gate, 1, 2), jnp.swapaxes(w_up, 1, 2)
        out_flat = w_out.reshape(w_out.shape[0], COLUMNS, width)
        flat = lambda w, layer: w[layer].reshape(width, COLUMNS)
        project_next = jnp.concatenate([flat(w, 1) for w in (w_query, w_key, w_value)], axis=1)
        prompt_pos = home * prompt_rows + jnp.arange(prompt_rows)

        cos, sin = rope_tables(jnp.concatenate([prompt_pos, prompt_len + jnp.arange(resp_len)]))
        info = jnp.concatenate([
            targets[0].reshape(per, groups).T[:, None, :],
            jnp.broadcast_to(resp_lens[0], (groups, groups - 1, per)).astype(jnp.int32)], axis=1)
        mixed, res, infos, prompt = first_attention(
            x_prompt, x_resp[0], flat(w_query, 0), flat(w_key, 0), flat(w_value, 0), attn_gain[0], cos, sin, info, 0)
        lens = infos[:, 1, 0]
        need = (lens + groups - 1) // groups
        ends = jnp.sum(jnp.where(jnp.arange(groups)[:, None] >= jnp.arange(groups), need, 0), axis=1)
        starts = ends - need
        dealt = groups * per

        def finish_with(size, ident):
            def run(operands):
                mixed, res, prompt = operands
                slot = jnp.arange(size)
                which = jnp.sum((slot[:, None] >= ends).astype(jnp.int32), axis=1)
                row = slot - jnp.sum(jnp.where(which[:, None] == jnp.arange(groups), starts, 0), axis=1)
                real = slot < ends[-1]
                chosen = jnp.where(real, which * per + row, -1)[:, None] == jnp.arange(dealt)
                pick = chosen.astype(BF16)

                def pack(rows):
                    return jnp.dot(pick, rows, preferred_element_type=F32).astype(BF16)

                kept = pack(jnp.concatenate([mixed.reshape(dealt, COLUMNS), res.reshape(dealt, COLUMNS)], axis=1))
                rows = jnp.concatenate([prompt, kept], axis=0)
                tables = rope_tables(jnp.concatenate([prompt_pos, prompt_len + groups * row + home]))
                qkv, new_res = mega(
                    by_chunk(rows[:, :COLUMNS]), to_blocks(rows[:, COLUMNS:]), mlp_gain[0], attn_gain[1], [by_chunk(t) for t in tables],
                    out_flat, gate_t, up_t, w_down, project_next, 0, ident)
                qkv = qkv.reshape(prompt_rows + size, 3 * COLUMNS)
                part = per // RING
                back = jnp.where(real, (row // part) * (groups * part) + which * part + row % part, -1)
                place = (jnp.arange(dealt)[:, None] == back).astype(BF16)
                home_rows = jnp.dot(place, qkv[prompt_rows:], preferred_element_type=F32).astype(BF16)
                kv_prompt = jnp.stack([qkv[:prompt_rows, COLUMNS:PAIR * COLUMNS], qkv[:prompt_rows, PAIR * COLUMNS:]])
                mixed = second_attention(home_rows.reshape(RING, groups, part, 3 * COLUMNS), kv_prompt, ident + 1)
                wanted = jnp.sum(jnp.where(chosen, infos[:, 0, :].reshape(dealt), 0), axis=1) - me * w_vocab.shape[1]
                stats, _ = mega(
                    by_chunk(pack(mixed.reshape(dealt, COLUMNS))), to_blocks(from_blocks(new_res)[prompt_rows:]), mlp_gain[1], final_gain,
                    [by_chunk(jnp.broadcast_to(wanted[:, None], (size, LANES)))], out_flat, gate_t, up_t, w_down, w_vocab, 1, ident + PAIR)
                stats = jnp.pad(stats.reshape(size, LANES)[:, :3].T, ((0, 0), (0, dealt - size)))
                found = combine(stats.reshape(3, groups, per), shards, ident + 3).reshape(groups, dealt)
                start = jnp.sum(jnp.where(jnp.arange(groups) == home, starts, 0))
                mine = lax.dynamic_slice(jnp.pad(found, ((0, 0), (0, per))), (0, start), (groups, per))
                return mine.T.reshape(resp_len)
            return run

        index = sum((ends[-1] > size).astype(jnp.int32) for size in VARIANTS[:-1])
        log_probs = lax.switch(index, [finish_with(size, 1 + RING * i) for i, size in enumerate(VARIANTS)], (mixed, res, prompt))
        log_probs = jnp.where(jnp.arange(resp_len) < resp_lens[0], log_probs, 0.0)
        return log_probs[None, :]

    return jax.shard_map(device_step, mesh=mesh, in_specs=in_specs, out_specs=P(row_axes, None), check_vma=False)
```

profile of v0, /device:TPU:1, one launch (start us, length us, event | category | flops | bytes accessed | tf_op | source)
XLA Modules:
  0.0 655.2 jit_solution(2910784576373535270)
XLA Ops:
  0.0 2.1 fusion.54
  2.2 1.5 pad_maximum_fusion.17
  3.6 3.8 fusion.59
  7.4 3.8 fusion.60
  11.2 2.9 copy_bitcast_fusion.11
  14.4 3.8 fusion.58
  18.1 1.6 copy.99
  23.0 37.1 %first_attention.1 = (bf16[8,4,32,256]{3,2,1,0:T(8,128)(2,1)}, bf16[8,8,16,256]{3,2,1,0:T(8,128)(2,1)}, s32[8,8,128]{2,1,0:T(8,128)S(1)}, bf16[128,512]{1,0:T(8,128)(2,1)}) custom-call(bf16[128,4096]{1,0:T(8,128)(2,1)} %xp_hbm.1, bf16[1024,4096]{1,0:T(8,128)(2,1)} %bitcast.161, bf16[4096,256]{1,0:T(8,128)(2,1)} %bitcast.162, ...), custom_call_target="tpu_custom_call" | custom-call | tf_op jit(solution)/shard_map/first_attention/pallas_call | solution.py:629
  60.5 3.0 copy_bitcast_fusion.8
  63.9 3.0 pad_maximum_fusion.16
  66.9 0.7 slice.104
  68.3 585.6 %conditional.1 = (f32[1024]{0:T(1024)S(1)}) conditional(s32[]{:T(128)} %bitcast.76, (s32[8]{0:T(128)S(1)}, s32[8]{0:T(128)S(1)}, bf16[8,4,32,256]{3,2,1,0:T(8,128)(2,1)S(1)}, bf16[8,8,16,256]{3,2,1,0:T(8,128)(2,1)S(1)}, bf16[128,512]{1,0:T(8,128)(2,1)S(1)}, /*index=5*/f32[2,4096]{1,0:T(2,128)S(1)}, f32[2,4096]{1,0:T(2,128)}, s32[128]{0:T(128)S(1)}, ...), branch_computations={%region_1.6_spmd, %region_6.11_spmd} | conditional | flops 3234170368 | bytes 28216982 | solution.py:839
  68.9 1.6 fusion.14
  70.5 1.2 pad_maximum_fusion.1
  72.9 1.0 fusion.7
  73.9 0.8 pad_maximum_fusion
  74.8 0.8 copy.91
  75.6 0.8 slice.70
  77.1 245.2 %mega1.1 = (bf16[4,2,104,768]{3,2,1,0:T(8,128)(2,1)}, bf16[4,2,2,104,128]{4,3,2,1,0:T(8,128)(2,1)}) custom-call(bf16[4,2,104,256]{3,2,1,0:T(8,128)(2,1)} %bitcast.179, bf16[4,2,2,104,128]{4,3,2,1,0:T(8,128)(2,1)} %bitcast.178, f32[2,32,128]{2,1,0:T(8,128)} %get-tuple-element.143.gain_ref, f32[2,32,128]{2,1,0:T(8,128)} %get-tuple-element.144.next_gain_ref, ...), custom_call_target="tpu_custom_call" | custom-call | tf_op jit(solution)/shard_map/cond/branch_0_fun/mega1/pallas_call | solution.py:369
  322.3 0.9 slice_bitcast_fusion.1
  323.2 0.7 pad_maximum_fusion.3.kv_prompt_ref
  323.8 3.9 fusion.3
  327.7 51.8 %second_attention2.1 = bf16[8,4,32,256]{3,2,1,0:T(8,128)(2,1)} custom-call(bf16[4,8,32,768]{3,2,1,0:T(8,128)(2,1)} %bitcast.180, bf16[2,128,256]{2,1,0:T(8,128)(2,1)} %pad_maximum_fusion.3.kv_prompt_ref), custom_call_target="tpu_custom_call" | custom-call | tf_op jit(solution)/shard_map/cond/branch_0_fun/second_attention2/pallas_call | solution.py:680
  379.5 2.5 fusion.8
  382.6 0.8 copy.92
  383.4 0.8 slice.76
  384.8 0.9 broadcast_in_dim.66.args_0_
  386.4 226.3 %mega3.1 = (f32[4,2,88,128]{3,2,1,0:T(8,128)}, bf16[4,2,2,88,128]{4,3,2,1,0:T(8,128)(2,1)}) custom-call(bf16[4,2,88,256]{3,2,1,0:T(8,128)(2,1)} %bitcast.190, bf16[4,2,2,88,128]{4,3,2,1,0:T(8,128)(2,1)} %bitcast.183, f32[2,32,128]{2,1,0:T(8,128)} %get-tuple-element.145.gain_ref, f32[2,32,128]{2,1,0:T(8,128)} %get-tuple-element.146.next_gain_ref, ...), custom_call_target="tpu_custom_call" | custom-call | tf_op jit(solution)/shard_map/cond/branch_0_fun/mega3/pallas_call | solution.py:369
  612.6 1.1 copy.64
  614.4 26.9 %combine4.1 = f32[8,8,128]{2,1,0:T(8,128)} custom-call(f32[3,8,128]{2,1,0:T(8,128)} %bitcast.218), custom_call_target="tpu_custom_call" | custom-call | tf_op jit(solution)/shard_map/cond/branch_0_fun/combine4/pallas_call | solution.py:732
  641.2 1.0 copy.62
  642.2 0.7 fusion.25
  (73 shorter events, 9.2 us)
Async XLA Ops:
  0.0 3.6 copy-start.1
  3.6 3.8 copy-start.2
  11.2 3.1 copy-start.3
  18.1 2.8 copy-start.14
  18.1 4.2 copy-start.11
  60.1 3.5 copy-start.13
  60.5 3.1 copy-start
  63.8 4.4 copy-start.5
  63.8 4.4 copy-start.7
  63.9 4.4 copy-start.8
  63.9 4.4 copy-start.19
  63.9 4.4 copy-start.22
  68.3 0.5 copy-start.15
  379.5 2.5 copy-start.6
  386.3 255.9 %copy-start.16 = (s32[8]{0:T(128)S(1)}, s32[8]{0:T(128)}, u32[]{:S(2)}) copy-start(s32[8]{0:T(128)} %copy-done.15) | copy-start | bytes 100 | tf_op jit(solution)/shard_map/cond
where the time goes:
time: 663 us; the launch traced here: 655 us
  Pallas kernels  587 us (89%)
  local copies, waits for them, and re-layouts  31.6 us (5%)
  other arithmetic  15.7 us (2%)
  loops' own time  11 us (2%)
  matrix products  7.34 us (1%)
    pallas_call x2, Pallas kernels, mega(): pl.pallas_call(functools.partial(mega_kernel, chunks, layer, last), out_s...  471 us
    pallas_call x1, Pallas kernels, second_attention(): pl.pallas_call(second_attention_kernel, out_shape=jax.ShapeDtypeStruct((P...  51.8 us
    pallas_call x1, Pallas kernels, first_attention(): pl.pallas_call(first_attention_kernel, out_shape=(jax.ShapeDtypeStruct((P...  37.1 us
    pallas_call x1, Pallas kernels, combine(): pl.pallas_call(functools.partial(combine_kernel, shards), out_shape=jax.S...  26.9 us

commit v1 on v0

--- a/solution.py
+++ b/solution.py
@@ -20,8 +20,6 @@
 VMEM_BYTES = 67_000_000
 LATE_ROWS = 640
 LOGITS = 512
-GROUP = 2
-LAG = 4
 VMEM = pl.BlockSpec(memory_space=pltpu.VMEM)
 ANY = pl.BlockSpec(memory_space=pl.ANY)
 DMA = pltpu.SemaphoreType.DMA
@@ -246,29 +244,29 @@
     return jnp.concatenate([v * cos + pltpu.roll(v, LANES // PAIR, 1) * sin for v in halves(value)], axis=1)
 
 
-def put_projected(product, cos_ref, sin_ref, out_ref, c, q):
+def put_projected(product, cos_ref, sin_ref, out_ref, c):
     for k in range(3):
         value = product(k * COLUMNS, COLUMNS)
         if k < PAIR:
-            value = rope(value, cos_ref[c, q], sin_ref[c, q])
-        out_ref[c, q, :, pl.ds(k * COLUMNS, COLUMNS)] = value.astype(BF16)
-
-
-def put_statistics(product, count, target_ref, out_ref, c, q):
+            value = rope(value, cos_ref[c], sin_ref[c])
+        out_ref[c, :, pl.ds(k * COLUMNS, COLUMNS)] = value.astype(BF16)
+
+
+def put_statistics(product, count, target_ref, out_ref, c):
     top = total = picked = None
     for k in range(count // LOGITS):
         logits = product(k * LOGITS, LOGITS)
         here = jnp.max(logits, axis=-1, keepdims=True)
         ids = lax.broadcasted_iota(jnp.int32, logits.shape, 1) + k * LOGITS
-        found = jnp.sum(jnp.where(ids == target_ref[c, q, :, :1], logits, 0.0), axis=-1, keepdims=True)
+        found = jnp.sum(jnp.where(ids == target_ref[c, :, :1], logits, 0.0), axis=-1, keepdims=True)
         if k:
             both = jnp.maximum(top, here)
             total = total * jnp.exp(top - both) + jnp.sum(jnp.exp(logits - both), axis=-1, keepdims=True)
             top, picked = both, picked + found
         else:
             top, total, picked = here, jnp.sum(jnp.exp(logits - here), axis=-1, keepdims=True), found
-    lane = lax.broadcasted_iota(jnp.int32, out_ref.shape[PAIR:], 1)
-    out_ref[c, q] = jnp.where(lane == 0, top, jnp.where(lane == 1, total, picked))
+    lane = lax.broadcasted_iota(jnp.int32, out_ref.shape[1:], 1)
+    out_ref[c] = jnp.where(lane == 0, top, jnp.where(lane == 1, total, picked))
 
 
 def mega_kernel(chunks, layer, last, a_ref, res_ref, gain_ref, next_gain_ref, *args):
@@ -300,17 +298,21 @@
     first = Stage(net, lambda c, q: a_ref[c, q], w_out, finish_with(res_ref, middle))
     second = Stage(net, lambda c, q: inner[c, q], w_down, finish_with(middle, new_res_ref))
 
-    def mlp(c, q):
-        first.complete(c, q)
-        normed(net, c, q, gain_ref)
-        hidden = rows_of(net, c, q)
-        inner[c, q] = (jax.nn.silu(times_transposed(hidden, w_gate[...])) * times_transposed(hidden, w_up[...])).astype(BF16)
-        second.begin(c, q)
-
-    def after(c, q):
-        second.complete(c, q)
-        normed(net, c, q, next_gain_ref)
-        hidden = rows_of(net, c, q)
+    def hidden_of(c, stage, gain):
+        for q in BOTH:
+            stage.complete(c, q)
+            normed(net, c, q, gain)
+        return jnp.concatenate([rows_of(net, c, q) for q in BOTH], axis=0)
+
+    def mlp(c):
+        hidden = hidden_of(c, first, gain_ref)
+        value = (jax.nn.silu(times_transposed(hidden, w_gate[...])) * times_transposed(hidden, w_up[...])).astype(BF16)
+        inner[c] = value.reshape(inner.shape[1:])
+        for q in BOTH:
+            second.begin(c, q)
+
+    def after(c):
+        hidden = hidden_of(c, second, next_gain_ref)
 
         def product(lane, size):
             parts = [jnp.dot(hidden[:, start:start + rows_here], (w_gate, w_up)[buffer][pl.ds(0, rows_here), pl.ds(at + lane, size)], preferred_element_type=F32)
@@ -320,35 +322,42 @@
             return functools.reduce(jnp.add, parts)
 
         if last:
-            put_statistics(product, count, *side_refs, out_ref, c, q)
+            put_statistics(product, count, *side_refs, out_ref, c)
         else:
-            put_projected(product, *side_refs, out_ref, c, q)
-
-    steps = [first.begin, *first.middle(), mlp, *second.middle(), after]
-    groups = [(at, min(at + GROUP, chunks)) for at in range(0, chunks, GROUP)]
-    final = len(groups) - 1
-
-    def run(step, group):
-        if step == mlp and group == 0:
+            put_projected(product, *side_refs, out_ref, c)
+
+    def on_both(step):
+        def run(c):
+            for q in BOTH:
+                step(c, q)
+        return run
+
+    steps = [on_both(first.begin), *map(on_both, first.middle()), mlp, *map(on_both, second.middle()), after]
+    at_mlp = steps.index(mlp)
+
+    @pl.loop(0, len(steps) + chunks - 1)
+    def _(slot):
+        @pl.when(slot == at_mlp)
+        def _():
             for load in loads[1:]:
                 load.wait()
-        if step == after and group == 0:
+
+        @pl.when(slot == len(steps) - 1)
+        def _():
             for load in late_loads:
                 load.wait()
 
-        @pl.loop(*groups[group])
-        def _(c):
-            for q in BOTH:
-                step(c, q)
-
-        if step == mlp and group == final:
+        for k, step in reversed(list(enumerate(steps))):
+            @pl.when(slot >= k)
+            def _():
+                @pl.when(slot < k + chunks)
+                def _():
+                    step(slot - k)
+
+        @pl.when(slot == at_mlp + chunks - 1)
+        def _():
             for load in late_loads:
                 load.start()
-
-    for slot in range(len(steps) + LAG * final):
-        for group in range(len(groups)):
-            if 0 <= slot - LAG * group < len(steps):
-                run(steps[slot - LAG * group], group)
 
 
 def mega(a, res, gain, next_gain, sides, w_out, w_gate_t, w_up_t, w_down, late, layer, collective_id):
@@ -365,7 +374,7 @@
         return jnp.stack([jnp.swapaxes(grid, 0, 1), grid]).reshape(PAIR, PAIR * SHARDS, LANES)
 
     sem = DMA(per + (PAIR, len(KINDS)))
-    out = jax.ShapeDtypeStruct(per + tile, F32) if last else jax.ShapeDtypeStruct(per + (rows, count), BF16)
+    out = jax.ShapeDtypeStruct((chunks, PAIR * rows, LANES if last else count), F32 if last else BF16)
     return pl.pallas_call(
         functools.partial(mega_kernel, chunks, layer, last),
         out_shape=(out, jax.ShapeDtypeStruct(per + (PAIR,) + tile, BF16)),
@@ -540,7 +549,7 @@
 
 def first_attention_kernel(xp_hbm, xr_hbm, wq_hbm, wk_hbm, wv_hbm, gain_ref, cos_ref, sin_ref, info_ref,
                            mixed_out, res_out, info_out, prompt_out,
-                           xs, w, hidden, q_s, k_s, v_s, held, mixed_stage, res_stage,
+                           xs, w, even, odd, q_s, k_s, v_s, held, mixed_stage, res_stage,
                            x_sem, w_sem, ring_send, ring_recv, near_send, near_recv, mix_send, mix_recv, res_send, res_recv, info_send, info_recv):
     net = Exchange()
     prompt = PromptGather(net, held, ring_send, ring_recv, near_send, near_recv)
@@ -561,43 +570,47 @@
     net.scatter(lambda d: info_ref.at[d], info_out.at[me], info_send, info_recv)
     info_out[me] = info_ref[me]
 
-    def project(t):
+    def project(t, hidden):
         span = pl.ds(pl.multiple_of(t * TILE, TILE), TILE)
-        qkv = jnp.dot(hidden[t % 2], w[...], preferred_element_type=F32)
+        qkv = jnp.dot(hidden[...], w[...], preferred_element_type=F32)
         cos, sin = cos_ref[span], sin_ref[span]
         return span, rope(qkv[:, :COLUMNS], cos, sin).astype(BF16), rope(qkv[:, COLUMNS:512], cos, sin).astype(BF16), qkv[:, 512:].astype(BF16)
 
     load(0).wait()
-    norm_tile(xs.at[0], hidden.at[0], gain_ref)
-    load(1).wait()
+    norm_tile(xs.at[0], even, gain_ref)
     for copy in weights:
         copy.wait()
-    norm_tile(xs.at[1], hidden.at[1], gain_ref)
-    span, q, k, v = project(0)
+    load(1).wait()
+    span, q, k, v = project(0, even)
+    norm_tile(xs.at[1], odd, gain_ref)
     q_s[span] = q
     held[me, 0] = k
     held[me, 1] = v
     prompt.start()
     spread = deal(TILE)
 
-    @pl.loop(1, 9)
-    def _(t):
-        later = jnp.minimum(t + 1, 8)
-
-        @pl.when(t < 8)
-        def _():
-            load(t + 1).wait()
-
-        span, q, k, v = project(t)
-        norm_tile(xs.at[later], hidden.at[(t + 1) % 2], gain_ref)
+    def response_tile(t, here, there):
+        span, q, k, v = project(t, here)
+        norm_tile(xs.at[jnp.minimum(t + 1, 8)], there, gain_ref)
         q_s[span] = q
         own = pl.ds(pl.multiple_of((t - 1) * TILE, TILE), TILE)
         k_s[own] = k
         v_s[own] = v
         dealt = jnp.dot(spread, xs[t, :, pl.ds(column, COLUMNS)], preferred_element_type=F32).astype(BF16)
         res_stage[:, t - 1] = dealt.reshape(PEERS, TILE // PEERS, COLUMNS)
-        pl.when(t == 3)(prompt.relay)
-        pl.when(t == 5)(prompt.share)
+
+    @pl.loop(0, RING)
+    def _(i):
+        load(PAIR * i + PAIR).wait()
+        response_tile(PAIR * i + 1, odd, even)
+
+        @pl.when(i < RING - 1)
+        def _():
+            load(PAIR * i + 3).wait()
+
+        response_tile(PAIR * i + PAIR, even, odd)
+        pl.when(i == 1)(prompt.relay)
+        pl.when(i == PAIR)(prompt.share)
 
     net.scatter(lambda d: res_stage.at[d], res_out.at[me], res_send, res_recv)
     res_out[me] = res_stage[me]
@@ -633,7 +646,7 @@
         in_specs=[ANY] * 5 + [VMEM] * 4,
         out_specs=(VMEM,) * 4,
         scratch_shapes=[
-            pltpu.VMEM((9, TILE, width), BF16), pltpu.VMEM((width, 768), BF16), pltpu.VMEM((2, TILE, width), BF16),
+            pltpu.VMEM((9, TILE, width), BF16), pltpu.VMEM((width, 3 * COLUMNS), BF16), pltpu.VMEM((TILE, width), BF16), pltpu.VMEM((TILE, width), BF16),
             pltpu.VMEM((rows, COLUMNS), BF16), pltpu.VMEM((rows - TILE, COLUMNS), BF16), pltpu.VMEM((rows - TILE, COLUMNS), BF16),
             HELD, pltpu.VMEM((RING, PEERS, 32, COLUMNS), BF16), pltpu.VMEM((PEERS, 8, 16, COLUMNS), BF16),
             DMA((9,)), DMA((3,)), *GATHER_SEMS, DMA((RING, PEERS)), DMA((RING, PEERS)), *[DMA((PEERS,)) for _ in range(RING)],
@@ -741,7 +754,7 @@
 
 
 ROPE_BASE = 10000.0
-VARIANTS = (704, 1024)
+VARIANTS = (768, 1024)
 CHUNKS = 4
 
 
@@ -755,6 +768,10 @@
 
 def by_chunk(rows):
     return rows.reshape(CHUNKS, PAIR, rows.shape[0] // (CHUNKS * PAIR), rows.shape[1])
+
+
+def side(rows):
+    return rows.reshape(CHUNKS, -1, LANES)
 
 
 def to_blocks(rows):
@@ -815,7 +832,7 @@
                 rows = jnp.concatenate([prompt, kept], axis=0)
                 tables = rope_tables(jnp.concatenate([prompt_pos, prompt_len + groups * row + home]))
                 qkv, new_res = mega(
-                    by_chunk(rows[:, :COLUMNS]), to_blocks(rows[:, COLUMNS:]), mlp_gain[0], attn_gain[1], [by_chunk(t) for t in tables],
+                    by_chunk(rows[:, :COLUMNS]), to_blocks(rows[:, COLUMNS:]), mlp_gain[0], attn_gain[1], [side(t) for t in tables],
                     out_flat, gate_t, up_t, w_down, project_next, 0, ident)
                 qkv = qkv.reshape(prompt_rows + size, 3 * COLUMNS)
                 part = per // RING
@@ -827,7 +844,7 @@
                 wanted = jnp.sum(jnp.where(chosen, infos[:, 0, :].reshape(dealt), 0), axis=1) - me * w_vocab.shape[1]
                 stats, _ = mega(
                     by_chunk(pack(mixed.reshape(dealt, COLUMNS))), to_blocks(from_blocks(new_res)[prompt_rows:]), mlp_gain[1], final_gain,
-                    [by_chunk(jnp.broadcast_to(wanted[:, None], (size, LANES)))], out_flat, gate_t, up_t, w_down, w_vocab, 1, ident + PAIR)
+                    [side(jnp.broadcast_to(wanted[:, None], (size, LANES)))], out_flat, gate_t, up_t, w_down, w_vocab, 1, ident + PAIR)
                 stats = jnp.pad(stats.reshape(size, LANES)[:, :3].T, ((0, 0), (0, dealt - size)))
                 found = combine(stats.reshape(3, groups, per), shards, ident + 3).reshape(groups, dealt)
                 start = jnp.sum(jnp.where(jnp.arange(groups) == home, starts, 0))

time: 663 us -> 633 us (0.955)
  Pallas kernels: 587 us -> 557 us
    pallas_call x2, Pallas kernels: 471 us -> 448 us  [mega(): pl.pallas_call(functools.partial(mega_kernel, chunks, layer, last), out_s...]
where the time goes in v1:
time: 633 us; the launch traced here: 625 us
  Pallas kernels  557 us (88%)
  local copies, waits for them, and re-layouts  31.6 us (5%)
  other arithmetic  15.9 us (3%)
  loops' own time  10.3 us (2%)
  matrix products  7.48 us (1%)
    pallas_call x2, Pallas kernels, mega(): pl.pallas_call(functools.partial(mega_kernel, chunks, layer, last), out_s...  448 us
    pallas_call x1, Pallas kernels, second_attention(): pl.pallas_call(second_attention_kernel, out_shape=jax.ShapeDtypeStruct((P...  47 us
    pallas_call x1, Pallas kernels, first_attention(): pl.pallas_call(first_attention_kernel, out_shape=(jax.ShapeDtypeStruct((P...  38.3 us
    pallas_call x1, Pallas kernels, combine(): pl.pallas_call(functools.partial(combine_kernel, shards), out_shape=jax.S...  23.9 us

profile of v1, /device:TPU:1, one launch (start us, length us, event | category | flops | bytes accessed | tf_op | source)
XLA Modules:
  0.0 624.7 jit_solution(12401554616161241109)
XLA Ops:
  0.0 2.1 fusion.54
  2.2 1.5 pad_maximum_fusion.17
  3.6 3.8 fusion.59
  7.4 3.8 fusion.60
  11.2 2.9 copy_bitcast_fusion.11
  14.3 3.8 fusion.58
  18.1 1.6 copy.99
  22.8 38.3 %first_attention.1 = (bf16[8,4,32,256]{3,2,1,0:T(8,128)(2,1)}, bf16[8,8,16,256]{3,2,1,0:T(8,128)(2,1)}, s32[8,8,128]{2,1,0:T(8,128)S(1)}, bf16[128,512]{1,0:T(8,128)(2,1)}) custom-call(bf16[128,4096]{1,0:T(8,128)(2,1)} %xp_hbm.1, bf16[1024,4096]{1,0:T(8,128)(2,1)} %bitcast.160, bf16[4096,256]{1,0:T(8,128)(2,1)} %bitcast.161, ...), custom_call_target="tpu_custom_call" | custom-call | tf_op jit(solution)/shard_map/first_attention/pallas_call | solution.py:642
  61.5 3.0 copy_bitcast_fusion.8
  64.9 3.0 pad_maximum_fusion.16
  69.2 554.4 %conditional.1 = (f32[1024]{0:T(1024)S(1)}) conditional(s32[]{:T(128)} %bitcast.75, (s32[8]{0:T(128)S(1)}, s32[8]{0:T(128)S(1)}, bf16[8,4,32,256]{3,2,1,0:T(8,128)(2,1)S(1)}, bf16[8,8,16,256]{3,2,1,0:T(8,128)(2,1)S(1)}, bf16[128,512]{1,0:T(8,128)(2,1)S(1)}, /*index=5*/f32[2,4096]{1,0:T(2,128)S(1)}, f32[2,4096]{1,0:T(2,128)}, s32[128]{0:T(128)S(1)}, ...), branch_computations={%region_1.6_spmd, %region_6.11_spmd} | conditional | flops 3234170368 | bytes 24030814 | solution.py:856
  70.1 1.7 fusion.14
  71.7 1.3 pad_maximum_fusion.1
  73.6 0.6 add_select_fusion.2
  74.3 1.0 fusion.7
  75.3 0.8 pad_maximum_fusion
  76.2 0.8 copy.91
  77.1 0.8 slice.70
  78.5 237.5 %mega1.1 = (bf16[4,224,768]{2,1,0:T(8,128)(2,1)}, bf16[4,2,2,112,128]{4,3,2,1,0:T(8,128)(2,1)}) custom-call(bf16[4,2,112,256]{3,2,1,0:T(8,128)(2,1)} %bitcast.176, bf16[4,2,2,112,128]{4,3,2,1,0:T(8,128)(2,1)} %bitcast.177, f32[2,32,128]{2,1,0:T(8,128)} %get-tuple-element.143.gain_ref, f32[2,32,128]{2,1,0:T(8,128)} %get-tuple-element.144.next_gain_ref, ...), custom_call_target="tpu_custom_call" | custom-call | tf_op jit(solution)/shard_map/cond/branch_0_fun/mega1/pallas_call | solution.py:378
  316.1 0.9 slice_bitcast_fusion.1
  316.9 0.7 pad_maximum_fusion.3.kv_prompt_ref
  317.6 3.9 fusion.3
  321.5 47.0 %second_attention2.1 = bf16[8,4,32,256]{3,2,1,0:T(8,128)(2,1)} custom-call(bf16[4,8,32,768]{3,2,1,0:T(8,128)(2,1)} %bitcast.181, bf16[2,128,256]{2,1,0:T(8,128)(2,1)} %pad_maximum_fusion.3.kv_prompt_ref), custom_call_target="tpu_custom_call" | custom-call | tf_op jit(solution)/shard_map/cond/branch_0_fun/second_attention2/pallas_call | solution.py:693
  368.6 2.5 fusion.8
  371.7 0.8 copy.92
  372.5 0.8 slice.76
  374.0 0.9 broadcast_in_dim.66.args_0_
  375.5 210.7 %mega3.1 = (f32[4,192,128]{2,1,0:T(8,128)}, bf16[4,2,2,96,128]{4,3,2,1,0:T(8,128)(2,1)}) custom-call(bf16[4,2,96,256]{3,2,1,0:T(8,128)(2,1)} %bitcast.189, bf16[4,2,2,96,128]{4,3,2,1,0:T(8,128)(2,1)} %bitcast.180, f32[2,32,128]{2,1,0:T(8,128)} %get-tuple-element.145.gain_ref, f32[2,32,128]{2,1,0:T(8,128)} %get-tuple-element.146.next_gain_ref, ...), custom_call_target="tpu_custom_call" | custom-call | tf_op jit(solution)/shard_map/cond/branch_0_fun/mega3/pallas_call | solution.py:378
  586.2 1.1 copy.64
  588.0 23.9 %combine4.1 = f32[8,8,128]{2,1,0:T(8,128)} custom-call(f32[3,8,128]{2,1,0:T(8,128)} %bitcast.217), custom_call_target="tpu_custom_call" | custom-call | tf_op jit(solution)/shard_map/cond/branch_0_fun/combine4/pallas_call | solution.py:745
  611.9 1.0 copy.62
  612.8 0.7 fusion.25
  (73 shorter events, 9.3 us)
Async XLA Ops:
  0.0 3.6 copy-start.1
  3.6 3.8 copy-start.2
  11.2 3.1 copy-start.3
  18.1 2.7 copy-start.14
  18.1 4.1 copy-start.11
  61.1 3.5 copy-start.13
  61.5 3.1 copy-start
  64.9 4.3 copy-start.5
  64.9 4.3 copy-start.7
  64.9 4.3 copy-start.8
  64.9 4.2 copy-start.19
  64.9 4.2 copy-start.20
  69.4 0.6 copy-start.15
  368.6 2.6 copy-start.6
  375.5 237.3 %copy-start.16 = (s32[8]{0:T(128)S(1)}, s32[8]{0:T(128)}, u32[]{:S(2)}) copy-start(s32[8]{0:T(128)} %copy-done.15) | copy-start | bytes 100 | tf_op jit(solution)/shard_map/cond
